TPU v7x, 512 devices: a whole 4x8x8 slice. The times are simulated.
512 devices in a mesh: row: 16 (over z_lo, y), col: 32 (over x, z_hi, core).
Axes of the slice: x: 4, y: 8, z: 8 (z_hi: 4, z_lo: 2; z = z_hi * 2 + z_lo), core: 2. Of those that a mesh axis runs over, the one named last changes fastest.
Arguments:
- amplitudes: bfloat16 [4096, 262144], P(None, ('row', 'col')), may hold values from -6 to 6
- integrals: bfloat16 [256, 262144], P(None, ('row', 'col')), may hold values from -6 to 6
- hh_coupling: bfloat16 [256, 4096], P('row'), may hold values from -0.09375 to 0.09375
- thc_factor: bfloat16 [512, 1024], P(None, ('row', 'col')), may hold values from -0.25 to 0.25
- thc_core: float32 [1024, 1024], P('col', 'row'), may hold values from -3 to 3
- occ_energy: float32 [64], replicated, may hold values from -2 to -0.5
- vir_energy: float32 [512], replicated, may hold values from 0.3 to 3
- pair_owner: int32 [256], replicated, may hold values from 0 to 4095, as said below
Outputs:
- updated: bfloat16 [256, 262144], P(None, ('row', 'col'))
Inputs may be any that keep to these rules, and one draw needn't show every extreme that they name: pair_owner holds 256 distinct occupied pairs.
All inputs are finite; a program needn't handle non-finite values.
Results may differ from a plain program's by a relative error of at most 0.007.
Values may be sent and summed in bfloat16 or wider, within the bound.
A program may use at most 64 MiB of HBM per device.

v0:
```python
import jax
import jax.numpy as jnp
from jax import lax
from jax.sharding import Mesh
from jax.sharding import PartitionSpec as P

ROW = ("row_0", "row_1")
ROW_COL = ("row_0", "row_1", "col")


def in_order(pieces, dim):
    pieces = jnp.moveaxis(pieces, 0, dim)
    dims = pieces.shape
    return pieces.reshape(*dims[:dim], dims[dim] * dims[dim + 1], *dims[dim + 2 :])


def sent_to_all(shard, axis):
    count = lax.axis_size(axis)
    return lax.all_to_all(
        jnp.broadcast_to(shard[None], (count, *shard.shape)), axis, 0, 0, tiled=True
    )


def gather_directly(shard, axis, dim):
    return in_order(sent_to_all(shard, axis), dim)


def gather_in_order(shard, axes, order):
    pieces = shard[None]
    for k in order:
        pieces = lax.all_gather(pieces, axes[k], axis=0, tiled=True)
    carried = [lax.axis_size(axes[k]) for k in reversed(order)]
    pieces = pieces.reshape(*carried, *shard.shape)
    turned = sorted(range(len(order)), key=lambda place: order[len(order) - 1 - place])
    return pieces.transpose(*turned, *range(len(order), pieces.ndim)).reshape(-1, *shard.shape)


def gathered_by_axis(shard, axes, order, dim):
    return in_order(gather_in_order(shard, axes, order), dim)


def cut_along(shard, dim, count):
    dims = shard.shape
    pieces = shard.reshape(*dims[:dim], count, dims[dim] // count, *dims[dim + 1 :])
    return jnp.moveaxis(pieces, dim, 0)


def exchange_both(shard, axis, axes, splits, concats):
    sizes = [lax.axis_size(a) for a in axes]
    pieces = cut_along(shard, splits[0], sizes[0])
    pieces = jnp.moveaxis(cut_along(pieces, splits[1] + 1, sizes[1]), 0, 1)
    inside = pieces.shape[2:]
    pieces = pieces.reshape(-1, *inside)
    pieces = lax.all_to_all(pieces, axis, split_axis=0, concat_axis=0, tiled=True)
    pieces = in_order(pieces.reshape(*sizes, *inside), concats[0] + 1)
    return in_order(pieces, concats[1])


def per_device(
    amplitudes, integrals, hh_coupling, thc_factor, thc_core, occ_energy, vir_energy, pair_owner
):
    row_count = lax.axis_size(ROW)
    col_count = lax.axis_size("col")
    row_index = lax.axis_index(ROW)
    col_index = lax.axis_index("col")
    virtual = vir_energy.shape[0]
    column_width = amplitudes.shape[1]
    orb_block = column_width // virtual
    pairs_all = pair_owner.shape[0]
    pairs_col = pairs_all // col_count
    occupied = occ_energy.shape[0]
    factor = lax.all_gather(thc_factor, ROW_COL, axis=1, tiled=True)
    points = factor.shape[1]
    block_points = points // row_count
    core_block = gather_directly(thc_core, "col", 0)
    owned = amplitudes[pair_owner]
    coupled = jnp.dot(
        gathered_by_axis(hh_coupling, ROW, (0, 1), 0),
        amplitudes,
        preferred_element_type=jnp.float32,
    )
    local_half = jnp.einsum(
        "pkd,dq->pkq",
        owned.reshape(pairs_all, orb_block, virtual),
        factor,
        preferred_element_type=jnp.float32,
    ).astype(jnp.bfloat16)
    sectioned = local_half.reshape(col_count, pairs_col, 1, 1, orb_block, row_count, block_points)
    moved = exchange_both(sectioned, ROW_COL, (ROW, "col"), (5, 0), (2, 3))
    half = moved.reshape(pairs_col, virtual, block_points)
    middle = jnp.einsum("cP,pcq->pPq", factor, half, preferred_element_type=jnp.float32)
    weighted = (core_block[None] * middle).astype(jnp.bfloat16)
    back = jnp.einsum("aP,pPq->paq", factor, weighted, preferred_element_type=jnp.float32).astype(
        jnp.bfloat16
    )
    vir_slice = virtual // row_count
    sectioned_back = back.reshape(pairs_col, row_count, vir_slice, block_points)
    gathered_back = lax.all_to_all(sectioned_back, ROW, split_axis=1, concat_axis=3, tiled=True)
    gathered_back = gathered_back.reshape(pairs_col, vir_slice, row_count, block_points)
    factor_split = factor.reshape(virtual, row_count, block_points)
    partial_value = jnp.einsum(
        "parq,brq->rapb", gathered_back, factor_split, preferred_element_type=jnp.float32
    ).astype(jnp.bfloat16)
    ladder = jnp.sum(partial_value.astype(jnp.float32), axis=0).astype(jnp.bfloat16)
    ladder = ladder.reshape(col_count, orb_block, pairs_col, virtual)
    returned = lax.all_to_all(ladder, "col", split_axis=0, concat_axis=2, tiled=True)
    returned = (
        returned.reshape(orb_block, pairs_all, virtual)
        .transpose(1, 0, 2)
        .reshape(pairs_all, column_width)
    )
    device = row_index * col_count + col_index
    vir_mine = lax.dynamic_slice_in_dim(vir_energy, device * orb_block, orb_block, 0)
    orbital_ids = jnp.arange(occupied, dtype=jnp.int32)
    first_hit = (pair_owner // occupied)[:, None] == orbital_ids[None, :]
    second_hit = (pair_owner % occupied)[:, None] == orbital_ids[None, :]
    first_occ = jnp.sum(jnp.where(first_hit, occ_energy[None, :], 0.0), axis=1)
    second_occ = jnp.sum(jnp.where(second_hit, occ_energy[None, :], 0.0), axis=1)
    vir_pairs = vir_mine[:, None] + vir_energy[None, :]
    denom = vir_pairs - (first_occ + second_occ)[:, None]
    rest = integrals.astype(jnp.float32) + coupled + returned.astype(jnp.float32)
    update = 0.4 * owned.astype(jnp.float32) + 0.6 * rest / denom
    return update.astype(jnp.bfloat16)


def solution(mesh):
    finer = Mesh(mesh.devices.reshape(2, 8, mesh.shape["col"]), ("row_0", "row_1", "col"))
    in_specs = (
        P(None, ROW_COL),
        P(None, ROW_COL),
        P(ROW, None),
        P(None, ROW_COL),
        P("col", ROW),
        P(),
        P(),
        P(),
    )
    out_specs = P(None, ROW_COL)
    return jax.shard_map(
        per_device, mesh=finer, in_specs=in_specs, out_specs=out_specs, check_vma=False
    )
```

profile of v0, /device:TPU:1, one launch (start us, length us, event | category | flops | bytes accessed | tf_op | source)
XLA Modules:
  0.0 883.5 jit_solution(17219511499074198008)
XLA Ops:
  6.5 0.7 all-gather.7.cloned.1.call-update
  7.3 0.8 broadcast_in_dim.39
  8.0 1.0 reshape.74
  9.1 14.5 %all-to-all-start = ((f32[32,1,2048]{2,1,0:T(1,128)}), f32[32,1,2048]{2,1,0:T(1,128)}, u32[]{:S(2)}, u32[]{:S(2)}) async-start(f32[32,1,2048]{2,1,0:T(1,128)} %reshape.74), calls=%async_computation | async-start | bytes 524288 | tf_op jit(solution)/shard_map/all_to_all | solution.py:19
  23.6 10.7 %all-gather = bf16[32,4096]{1,0:T(8,128)(2,1)} all-gather(bf16[16,4096]{1,0:T(8,128)(2,1)} %param.10), channel_id=2, replica_groups=mesh['row_0'=2,'row_1'=8,'col'=32] {'row_0'}, dimensions={0}, use_global_device_ids=true | all-gather | bytes 393216 | tf_op jit(solution)/shard_map/all_gather | solution.py:31
  34.4 3.9 gather_fusion
  38.3 741.5 %all-gather.7.cloned.1.call-done = bf16[512,2,512]{2,1,0:T(2,128)(2,1)} async-done(((bf16[1,2,512]{2,1,0:T(2,128)(2,1)}), bf16[512,2,512]{2,1,0:T(2,128)(2,1)}) %all-gather.7.cloned.1.call-update) | async-done | bytes 1048592 | tf_op jit(solution)/shard_map/all_gather | solution.py:72
  779.8 1.5 reshape.68
  781.8 0.7 reshape_reshape.13
  782.7 1.4 reshape.72
  784.2 12.4 %all-to-all-start.1 = ((bf16[512,2,256]{2,1,0:T(2,128)(2,1)}), bf16[512,2,256]{2,1,0:T(2,128)(2,1)S(1)}, u32[]{:S(2)}, u32[]{:S(2)}) async-start(bf16[512,2,256]{2,1,0:T(2,128)(2,1)} %reshape.72), calls=%async_computation.1 | async-start | bytes 1048576 | tf_op jit(solution)/shard_map/all_to_all | solution.py:54
  797.1 2.9 reduce.2
  800.0 1.1 reshape.75
  801.2 0.9 copy.38
  802.1 1.2 reshape.69
  803.3 20.9 %all-to-all-done.1 = bf16[512,2,256]{2,1,0:T(2,128)(2,1)S(1)} async-done(((bf16[512,2,256]{2,1,0:T(2,128)(2,1)}), bf16[512,2,256]{2,1,0:T(2,128)(2,1)S(1)}, u32[]{:S(2)}, u32[]{:S(2)}) %all-to-all-start.1) | async-done | bytes 524320 | tf_op jit(solution)/shard_map/all_to_all | solution.py:54
  824.2 0.6 reshape.73
  824.8 1.0 bitcast_bitcast_fusion
  825.9 0.5 copy-done.1
  826.4 4.2 fusion.1
  830.6 1.5 copy.43
  832.2 0.7 reshape.76
  833.0 15.6 %all_to_all.34 = bf16[16,2,8192]{2,1,0:T(2,128)(2,1)S(1)} all-to-all(bf16[16,2,8192]{2,1,0:T(2,128)(2,1)S(1)} %reshape.76), channel_id=1, replica_groups=mesh['row_0'=2,'row_1'=8,'col'=32] {'row_0','row_1'}, dimensions={0} | all-to-all | bytes 1048576 | tf_op jit(solution)/shard_map/all_to_all | solution.py:98
  848.5 0.7 reshape.77
  849.2 1.2 convert_reduce_fusion
  850.4 0.9 copy.45
  851.3 7.9 all-to-all-start.3
  859.2 0.7 dynamic_slice.3
  860.0 0.6 broadcast_add_fusion
  860.7 1.8 copy.37
  862.4 10.0 %all-to-all-done.3 = bf16[32,1,8,512]{3,2,1,0:T(8,128)(2,1)S(1)} async-done(((bf16[32,1,8,512]{3,2,1,0:T(8,128)(2,1)}), bf16[32,1,8,512]{3,2,1,0:T(8,128)(2,1)S(1)}, u32[]{:S(2)}, u32[]{:S(2)}) %all-to-all-start.3) | async-done | bytes 262176 | tf_op jit(solution)/shard_map/all_to_all | solution.py:106
  872.5 4.2 fusion.6
  (24 shorter events, 1.6 us)
Async XLA Ops:
  6.5 27.8 %copy-start.3 = (s32[256]{0:T(256)S(1)}, s32[256]{0:T(256)}, u32[]{:S(2)}) copy-start(s32[256]{0:T(256)} %param.15) | copy-start | bytes 3076
  6.5 773.3 %all-gather.7.cloned.1.call-start = ((), (), s32[]{:S(2)}) async-start(), calls=%async_computation.5 | async-start | bytes 1050624 | tf_op jit(solution)/shard_map/all_gather | solution.py:72
  9.1 775.1 %all-to-all-start = ((f32[32,1,2048]{2,1,0:T(1,128)}), f32[32,1,2048]{2,1,0:T(1,128)}, u32[]{:S(2)}, u32[]{:S(2)}) async-start(f32[32,1,2048]{2,1,0:T(1,128)} %reshape.74), calls=%async_computation | async-start | bytes 524288 | tf_op jit(solution)/shard_map/all_to_all | solution.py:19
  23.5 837.1 %all-gather.5.cloned.1.call-start = ((), (), s32[]{:S(2)}) async-start(), calls=%async_computation.4 | async-start | bytes 2359296 | tf_op jit(solution)/shard_map/all_gather | solution.py:31
  782.7 19.4 %copy-start = (bf16[512,2,512]{2,1,0:T(2,128)(2,1)S(1)}, bf16[512,2,512]{2,1,0:T(2,128)(2,1)}, u32[]{:S(2)}) copy-start(bf16[512,2,512]{2,1,0:T(2,128)(2,1)} %all-gather.7.cloned.1.call-done) | copy-start | bytes 3145732
  784.2 40.0 %all-to-all-start.1 = ((bf16[512,2,256]{2,1,0:T(2,128)(2,1)}), bf16[512,2,256]{2,1,0:T(2,128)(2,1)S(1)}, u32[]{:S(2)}, u32[]{:S(2)}) async-start(bf16[512,2,256]{2,1,0:T(2,128)(2,1)} %reshape.72), calls=%async_computation.1 | async-start | bytes 1048576 | tf_op jit(solution)/shard_map/all_to_all | solution.py:54
  824.8 1.6 copy-start.1
  849.2 10.0 %copy-start.2 = (f32[512]{0:T(512)S(1)}, f32[512]{0:T(512)}, u32[]{:S(2)}) copy-start(f32[512]{0:T(512)} %param.14) | copy-start | bytes 6148
  849.2 10.7 %copy-start.4 = (f32[64]{0:T(128)S(1)}, f32[64]{0:T(128)}, u32[]{:S(2)}) copy-start(f32[64]{0:T(128)} %param.13) | copy-start | bytes 772
  851.3 21.2 %all-to-all-start.3 = ((bf16[32,1,8,512]{3,2,1,0:T(8,128)(2,1)}), bf16[32,1,8,512]{3,2,1,0:T(8,128)(2,1)S(1)}, u32[]{:S(2)}, u32[]{:S(2)}) async-start(bf16[32,1,8,512]{3,2,1,0:T(8,128)(2,1)} %copy.45), calls=%async_computation.3 | async-start | bytes 524288 | tf_op jit(solution)/shard_map/all_to_all | solution.py:106
  860.7 11.8 %copy-start.5 = (bf16[256,512]{1,0:T(8,128)(2,1)S(1)}, bf16[256,512]{1,0:T(8,128)(2,1)}, u32[]{:S(2)}) copy-start(bf16[256,512]{1,0:T(8,128)(2,1)} %param.9) | copy-start | bytes 786436
Sparse Core Ops, SparseCore 0:
  9.5 770.3 all-gather.6
  781.9 45.5 all-gather.4
where the time goes:
time: 884 us
  waiting for transfers between devices  773 us (87%)
  starting transfers between devices  34.8 us (4%)
  blocking collectives  26.3 us (3%)
  local copies, waits for them, and re-layouts  21.9 us (2%)
  between operations  13.6 us (2%)
  matrix products  10.1 us (1%)
    all_gather x1, waiting for transfers between devices, per_device(): factor = lax.all_gather(thc_factor, ROW_COL, axis=1, tiled=True)  742 us
    all_to_all x1, waiting for transfers between devices, exchange_both(): lax.all_to_all(pieces, axis, split_axis=0, concat_axis=0, tiled=True)  20.9 us
  transfers between devices with their start and end apart: 5, of which 3 were waited for; matrix products, arithmetic and copies ran while one was open for 3% of the time, Pallas kernels for 0%

commit v1 on v0

v1 whole, which is shorter than its diff:
```python
import jax
import jax.numpy as jnp
from jax import lax
from jax.experimental import pallas as pl
from jax.experimental.pallas import tpu as pltpu
from jax.sharding import Mesh
from jax.sharding import PartitionSpec as P

AXES = ("zl", "y", "x", "zh", "core")
ROW = ("zl", "y")
COL = ("x", "zh", "core")
BF = jnp.bfloat16
F32 = jnp.float32
N_EXCHANGES = 24


def nt(a, b):
    return lax.dot_general(a, b, (((1,), (1,)), ((), ())), preferred_element_type=F32)


def nn(a, b):
    return jnp.dot(a, b, preferred_element_type=F32)


def iota(shape, dim):
    return lax.broadcasted_iota(jnp.int32, shape, dim)


def swap_matrix():
    i, j = iota((256, 256), 0), iota((256, 256), 1)
    return (j == (i % 16) * 16 + i // 16).astype(F32).astype(BF)


def order_matrix():
    p, c = iota((512, 512), 0), iota((512, 512), 1)
    return (c == (p % 16) * 32 + ((p // 16) % 16) * 2 + p // 256).astype(F32).astype(BF)


class Exchange:
    def __init__(self, sems, number, count, me, where, src, dst):
        self.send, self.recv = sems
        self.number, self.count, self.me = number, count, me
        self.where, self.src, self.dst = where, src, dst

    def copy(self, d, to, slot):
        return pltpu.make_async_remote_copy(
            src_ref=self.src(to),
            dst_ref=self.dst(slot),
            send_sem=self.send.at[self.number, d],
            recv_sem=self.recv.at[self.number, d],
            device_id=self.where(to),
            device_id_type=pl.DeviceIdType.MESH,
        )

    def each(self, act):
        def step(d, carry):
            act(d)
            return carry

        lax.fori_loop(1, self.count, step, 0)

    def start(self):
        def act(d):
            self.copy(d, lax.rem(self.me + d, self.count), self.me).start()

        self.each(act)

    def wait_recv(self):
        def act(d):
            source = lax.rem(self.me + self.count - d, self.count)
            self.copy(d, source, source).wait_recv()

        self.each(act)

    def wait_send(self):
        def act(d):
            self.copy(d, lax.rem(self.me + d, self.count), self.me).wait_send()

        self.each(act)


class RingOfFour:
    def __init__(self, sems, number, me, block, half):
        self.send, self.recv = sems
        self.number, self.me = number, me
        self.block, self.half = block, half

    def copy(self, part, ref, to):
        return pltpu.make_async_remote_copy(
            src_ref=ref,
            dst_ref=ref,
            send_sem=self.send.at[self.number, part],
            recv_sem=self.recv.at[self.number, part],
            device_id={"x": to},
            device_id_type=pl.DeviceIdType.MESH,
        )

    def members(self):
        return lax.rem(self.me + 1, 4), lax.rem(self.me + 2, 4), lax.rem(self.me + 3, 4)

    def start(self):
        right, _, left = self.members()
        self.copy(0, self.block(self.me), right).start()
        self.copy(1, self.block(self.me), left).start()

    def forward(self):
        right, _, left = self.members()
        self.copy(0, self.block(left), right).wait_recv()
        self.copy(2, self.half(left, 0), right).start()
        self.copy(1, self.block(right), left).wait_recv()
        self.copy(3, self.half(right, 1), left).start()

    def wait_recv(self):
        right, across, left = self.members()
        self.copy(2, self.half(across, 0), right).wait_recv()
        self.copy(3, self.half(across, 1), left).wait_recv()

    def wait_send(self):
        right, _, left = self.members()
        self.copy(0, self.block(self.me), right).wait_send()
        self.copy(1, self.block(self.me), left).wait_send()
        self.copy(2, self.half(left, 0), right).wait_send()
        self.copy(3, self.half(right, 1), left).wait_send()


class Swap:
    def __init__(self, sems, number, core, src, dst):
        self.send, self.recv = sems
        self.number, self.core = number, core
        self.src, self.dst = src, dst

    def copy(self, slot):
        return pltpu.make_async_remote_copy(
            src_ref=self.src,
            dst_ref=self.dst(slot),
            send_sem=self.send.at[self.number, 0],
            recv_sem=self.recv.at[self.number, 0],
            device_id={"core": 1 - self.core},
            device_id_type=pl.DeviceIdType.MESH,
        )

    def start(self):
        self.copy(self.core).start()

    def wait_recv(self):
        self.copy(1 - self.core).wait_recv()

    def wait_send(self):
        self.copy(self.core).wait_send()


def kernel(
    amp_hbm, integrals, hh, factor, core_in, occ, vir, owner, out,
    amp, own, own0, own1, in0, in1, mid0, mid1, fin0, fin1, whole,
    chunk, pieces, points, core_parts, core_block, rows, half, order0, order1,
    ladder, give, take, lad0, lad1, got0, got1, turn0, turn1, back0, back1,
    coupled, amp_sem, send_sems, recv_sems,
):
    zl, y, x, zh, core = (lax.axis_index(a) for a in AXES)
    r, xz = zl * 8 + y, x * 4 + zh
    other = 1 - core
    sems = (send_sems, recv_sems)
    MESH = pl.DeviceIdType.MESH

    def row_at(t):
        return {"zl": t // 8, "y": t % 8}

    def col_at(t):
        return {"x": t // 4, "zh": t % 4}

    def zh_at(t):
        return {"zh": t}

    fetch = pltpu.make_async_copy(amp_hbm, amp, amp_sem)
    fetch.start()

    barrier = pltpu.get_barrier_semaphore()

    def greet_row(d, carry):
        pl.semaphore_signal(
            barrier, inc=1, device_id=row_at(lax.rem(r + d, 16)), device_id_type=MESH
        )
        return carry

    def greet_col(d, carry):
        pl.semaphore_signal(
            barrier, inc=1, device_id=col_at(lax.rem(xz + d, 16)), device_id_type=MESH
        )
        return carry

    lax.fori_loop(1, 16, greet_row, 0)
    lax.fori_loop(1, 16, greet_col, 0)
    for d in range(4):
        pl.semaphore_signal(
            barrier,
            inc=1,
            device_id={"zh": lax.rem(zh + d, 4), "core": other},
            device_id_type=MESH,
        )

    for k in range(2):
        chunk[k] = factor[:, k * 256 : k * 256 + 256].astype(F32)
    core_parts[x, zh, r] = jnp.concatenate(
        [core_in[0:16, :], core_in[16:32, :]], axis=1
    ).astype(BF)
    tile = pl.ds(pl.multiple_of((core * 16 + xz) * 128, 128), 128)
    lanes = pl.ds(pl.multiple_of(zh * 128, 128), 128)
    rows[core, x, r, :, lanes] = hh[:, tile]
    swap = swap_matrix()

    pl.semaphore_wait(barrier, 34)

    def piece(d, c, to_zh, to_core, slot_zh, slot_core):
        return pltpu.make_async_remote_copy(
            src_ref=chunk.at[to_core],
            dst_ref=pieces.at[slot_zh, slot_core],
            send_sem=send_sems.at[0, d * 2 + c],
            recv_sem=recv_sems.at[0, d * 2 + c],
            device_id={"zh": to_zh, "core": to_core},
            device_id_type=MESH,
        )

    hops = [(d, c) for d in range(4) for c in range(2) if d or c]

    def piece_out(d, c):
        return piece(d, c, lax.rem(zh + d, 4), core if c == 0 else other, zh, core)

    def piece_in(d, c):
        from_zh, from_core = lax.rem(zh + 4 - d, 4), core if c == 0 else other
        return piece(d, c, from_zh, from_core, from_zh, from_core)

    for d, c in hops:
        piece_out(d, c).start()
    pieces[zh, core] = chunk[core]

    core_zh = Exchange(
        sems, 1, 4, zh, zh_at, lambda t: core_parts.at[x, zh, r], lambda s: core_parts.at[x, s, r]
    )
    core_row = Exchange(
        sems, 2, 16, r, row_at, lambda t: core_parts.at[x, :, r], lambda s: core_parts.at[x, :, s]
    )
    core_x = RingOfFour(
        sems, 3, x, lambda t: core_parts.at[t], lambda t, h: core_parts.at[t, pl.ds(h * 2, 2)]
    )
    fac_row = Exchange(
        sems, 4, 16, r, row_at, lambda t: points.at[core, r, x], lambda s: points.at[core, s, x]
    )
    fac_x = RingOfFour(
        sems,
        5,
        x,
        lambda t: points.at[core, :, t],
        lambda t, h: points.at[core, pl.ds(h * 8, 8), t],
    )
    fac_swap = Swap(sems, 6, core, points.at[core], lambda s: points.at[s])
    hh_row = Exchange(
        sems,
        7,
        16,
        r,
        row_at,
        lambda t: rows.at[core, x, r, :, lanes],
        lambda s: rows.at[core, x, s, :, lanes],
    )

    def lanes_of(t):
        return pl.ds(pl.multiple_of(t * 128, 128), 128)

    hh_zh = Exchange(
        sems,
        8,
        4,
        zh,
        zh_at,
        lambda t: rows.at[core, x, :, :, lanes],
        lambda s: rows.at[core, x, :, :, lanes_of(s)],
    )
    hh_x = RingOfFour(
        sems, 9, x, lambda t: rows.at[core, t], lambda t, h: rows.at[core, t, pl.ds(h * 8, 8)]
    )
    hh_swap = Swap(sems, 10, core, rows.at[core], lambda s: rows.at[s])
    amp0_row = Exchange(sems, 11, 16, r, row_at, lambda t: own0.at[t], lambda s: in0.at[s])
    amp1_col = Exchange(sems, 12, 16, xz, col_at, lambda t: own1.at[t], lambda s: in1.at[s])
    amp0_col = Exchange(sems, 13, 16, xz, col_at, lambda t: mid0.at[t], lambda s: fin0.at[s])
    amp1_row = Exchange(sems, 14, 16, r, row_at, lambda t: mid1.at[t], lambda s: fin1.at[s])
    amp_swap = Swap(sems, 15, core, whole.at[core], lambda s: whole.at[s])
    lad_swap = Swap(sems, 16, core, give, lambda s: take)
    lad0_col = Exchange(sems, 17, 16, xz, col_at, lambda t: lad0.at[t], lambda s: got0.at[s])
    lad1_row = Exchange(sems, 18, 16, r, row_at, lambda t: lad1.at[t], lambda s: got1.at[s])
    lad0_row = Exchange(sems, 19, 16, r, row_at, lambda t: turn0.at[t], lambda s: back0.at[s])
    lad1_col = Exchange(sems, 20, 16, xz, col_at, lambda t: turn1.at[t], lambda s: back1.at[s])

    core_zh.start()

    fetch.wait()
    own_f32 = coupled
    own_f32[...] = jnp.zeros((256, 512), F32)

    def pick(k, carry):
        hit = owner[...] == iota((256, 512), 1) + k * 512
        own_f32[...] += nn(
            hit.astype(F32).astype(BF), amp[pl.ds(pl.multiple_of(k * 512, 512), 512), :]
        )
        return carry

    lax.fori_loop(0, 8, pick, 0)
    own[...] = own_f32[...].astype(BF)
    own0[...] = own[:, :256].reshape(16, 16, 256)
    own1[...] = nn(swap, own[:, 256:]).astype(BF).reshape(16, 16, 256)
    amp0_row.start()
    amp1_col.start()
    in0[r] = own0[r]
    in1[xz] = own1[xz]

    for d, c in hops:
        piece_in(d, c).wait_recv()
    point = iota((16, 256), 0)
    tile16 = jnp.zeros((16, 256), F32)
    for a in range(4):
        for b in range(2):
            for j in range(2):
                tile16 = jnp.where(
                    point == a * 4 + b * 2 + j, pieces[a, b, pl.ds(j, 1), :], tile16
                )
    points[core, r, x] = tile16.astype(BF)
    fac_row.start()
    core_zh.wait_recv()
    core_row.start()
    hh_row.start()
    order = order_matrix()

    amp0_row.wait_recv()
    mid0[...] = nn(swap, in0[...].reshape(256, 256)).astype(BF).reshape(16, 16, 256)
    amp0_col.start()
    fin0[xz] = mid0[xz]
    amp1_col.wait_recv()
    mid1[...] = nn(swap, in1[...].reshape(256, 256)).astype(BF).reshape(16, 16, 256)
    amp1_row.start()
    fin1[r] = mid1[r]

    fac_row.wait_recv()
    fac_x.start()
    core_row.wait_recv()
    core_x.start()
    fac_x.forward()
    core_x.forward()
    hh_row.wait_recv()
    hh_zh.start()

    amp0_col.wait_recv()
    whole[core, :, :256] = fin0[...].reshape(256, 256)
    amp1_row.wait_recv()
    whole[core, :, 256:] = nn(swap, fin1[...].reshape(256, 256)).astype(BF)
    amp_swap.start()

    fac_x.wait_recv()
    fac_swap.start()
    hh_zh.wait_recv()
    hh_x.start()
    amp_swap.wait_recv()
    fac_swap.wait_recv()

    def all_points(h):
        return points[h].reshape(1024, 256)

    def my_points(h):
        return points[h, :, pl.ds(core * 2, 2)].reshape(512, 256)

    order0[...] = (nt(my_points(0), order[:, :256]) + nt(my_points(1), order[:, 256:])).astype(BF)
    order1[...] = (nt(order[:, :256], my_points(0)) + nt(order[:, 256:], my_points(1))).astype(BF)

    for h in range(4):
        at = pl.ds(h * 4, 4)
        got = nt(whole[...].reshape(512, 512)[:, :256], points[0, at].reshape(256, 256))
        got += nt(whole[...].reshape(512, 512)[:, 256:], points[1, at].reshape(256, 256))
        half[:, h * 256 : h * 256 + 256] = got.astype(BF)

    core_x.wait_recv()
    hh_x.forward()
    low = iota((256, 128), 1) < 64
    for t in range(8):
        even = core_parts[:, :, 2 * t].reshape(256, 128).astype(F32)
        odd = core_parts[:, :, 2 * t + 1].reshape(256, 128).astype(F32)
        first = jnp.where(low, even, pltpu.roll(odd, 64, 1))
        second = jnp.where(low, pltpu.roll(even, 64, 1), odd)
        core_block[:, 0, :, t * 128 : t * 128 + 128] = first.astype(BF).reshape(16, 16, 128)
        core_block[:, 1, :, t * 128 : t * 128 + 128] = second.astype(BF).reshape(16, 16, 128)

    for t in range(4):
        cols = slice(t * 256, t * 256 + 256)
        middle = nn(order0[...], half[:, cols])
        weighted = (core_block[:, :, :, cols].reshape(512, 256).astype(F32) * middle).astype(BF)
        back = nn(order1[...], weighted).astype(BF)
        at = pl.ds(t * 4, 4)
        for h in range(2):
            part = nn(back, points[h, at].reshape(256, 256))
            put = slice(h * 256, h * 256 + 256)
            if t == 0:
                ladder[:, put] = part
            else:
                ladder[:, put] += part

    give[...] = ladder[pl.ds(pl.multiple_of(other * 256, 256), 256), :].astype(BF)
    lad_swap.start()
    hh_x.wait_recv()
    hh_swap.start()
    lad_swap.wait_recv()
    mine = ladder[pl.ds(pl.multiple_of(core * 256, 256), 256), :] + take[...].astype(F32)
    mine = mine.astype(BF)
    lad0[...] = mine[:, :256].reshape(16, 16, 256)
    lad0_col.start()
    lad1[...] = nn(swap, mine[:, 256:]).astype(BF).reshape(16, 16, 256)
    lad1_row.start()
    got0[xz] = lad0[xz]
    got1[r] = lad1[r]

    hh_swap.wait_recv()
    coupled[...] = jnp.zeros((256, 512), F32)

    def couple(k, carry):
        coupled[...] += nn(
            rows[k // 4, k % 4].reshape(256, 512),
            amp[pl.ds(pl.multiple_of(k * 512, 512), 512), :],
        )
        return carry

    lad0_col.wait_recv()
    turn0[...] = nn(swap, got0[...].reshape(256, 256)).astype(BF).reshape(16, 16, 256)
    lad0_row.start()
    back0[r] = turn0[r]
    lad1_row.wait_recv()
    turn1[...] = nn(swap, got1[...].reshape(256, 256)).astype(BF).reshape(16, 16, 256)
    lad1_col.start()
    back1[xz] = turn1[xz]

    lax.fori_loop(0, 8, couple, 0)
    device = r * 32 + xz * 2 + core
    vir_mine = jnp.sum(
        jnp.where(iota((1, 512), 1) == device, vir[...], 0.0), axis=1, keepdims=True
    )
    orbital = iota((256, 64), 1)
    first_hit = (owner[...] // 64) == orbital
    second_hit = (owner[...] % 64) == orbital
    occ_first = jnp.sum(jnp.where(first_hit, occ[...], 0.0), axis=1, keepdims=True)
    occ_second = jnp.sum(jnp.where(second_hit, occ[...], 0.0), axis=1, keepdims=True)
    occ_pair = occ_first + occ_second

    def finish(cols, lad):
        denom = (vir_mine + vir[:, cols]) - occ_pair
        rest = integrals[:, cols].astype(F32) + coupled[:, cols] + lad.astype(F32)
        update = 0.4 * own[:, cols].astype(F32) + 0.6 * rest / denom
        out[:, cols] = update.astype(BF)

    lad0_row.wait_recv()
    finish(slice(0, 256), back0[...].reshape(256, 256))
    lad1_col.wait_recv()
    finish(slice(256, 512), nn(swap, back1[...].reshape(256, 256)))

    for d, c in hops:
        piece_out(d, c).wait_send()
    for move in (
        core_zh, core_row, core_x, fac_row, fac_x, fac_swap, hh_row, hh_zh, hh_x, hh_swap,
        amp0_row, amp1_col, amp0_col, amp1_row, amp_swap, lad_swap,
        lad0_col, lad1_row, lad0_row, lad1_col,
    ):
        move.wait_send()


def per_device(
    amplitudes, integrals, hh_coupling, thc_factor, thc_core, occ_energy, vir_energy, pair_owner
):
    vmem = pl.BlockSpec(memory_space=pltpu.VMEM)
    cube = pltpu.VMEM((16, 16, 256), BF)
    scratch = [
        pltpu.VMEM((4096, 512), BF),
        pltpu.VMEM((256, 512), BF),
        *[cube] * 8,
        pltpu.VMEM((2, 256, 512), BF),
        pltpu.VMEM((2, 2, 256), F32),
        pltpu.VMEM((4, 2, 2, 256), F32),
        pltpu.VMEM((2, 16, 4, 16, 256), BF),
        pltpu.VMEM((4, 4, 16, 16, 128), BF),
        pltpu.VMEM((16, 2, 16, 1024), BF),
        pltpu.VMEM((2, 4, 16, 16, 512), BF),
        pltpu.VMEM((512, 1024), BF),
        pltpu.VMEM((512, 512), BF),
        pltpu.VMEM((512, 512), BF),
        pltpu.VMEM((512, 512), F32),
        pltpu.VMEM((256, 512), BF),
        pltpu.VMEM((256, 512), BF),
        *[cube] * 8,
        pltpu.VMEM((256, 512), F32),
        pltpu.SemaphoreType.DMA,
        pltpu.SemaphoreType.DMA((N_EXCHANGES, 16)),
        pltpu.SemaphoreType.DMA((N_EXCHANGES, 16)),
    ]
    return pl.pallas_call(
        kernel,
        out_shape=jax.ShapeDtypeStruct((256, 512), BF),
        in_specs=[pl.BlockSpec(memory_space=pl.ANY)] + [vmem] * 7,
        out_specs=vmem,
        scratch_shapes=scratch,
        compiler_params=pltpu.CompilerParams(
            collective_id=0, has_side_effects=True, vmem_limit_bytes=48 * 1024 * 1024
        ),
    )(
        amplitudes,
        integrals,
        hh_coupling,
        thc_factor.T,
        thc_core,
        occ_energy.reshape(1, -1),
        vir_energy.reshape(1, -1),
        pair_owner.reshape(-1, 1),
    )


def solution(mesh):
    finer = Mesh(mesh.devices.reshape(2, 8, 4, 4, 2), AXES)
    wide = P(None, ROW + COL)
    in_specs = (wide, wide, P(ROW, None), wide, P(COL, ROW), P(), P(), P())
    return jax.shard_map(
        per_device, mesh=finer, in_specs=in_specs, out_specs=wide, check_vma=False
    )
```

time: 884 us -> 94.6 us (0.11)
  waiting for transfers between devices: 773 us -> 0 us
  Pallas kernels: 0 us -> 85.9 us
  starting transfers between devices: 34.8 us -> 0 us
  blocking collectives: 26.3 us -> 0 us
  local copies, waits for them, and re-layouts: 21.9 us -> 8.28 us
  between operations: 13.6 us -> 0.03 us
  matrix products: 10.1 us -> 0 us
    all_gather x2 -> x0, waiting for transfers between devices: 742 us -> none  [the longest x1 742 us: per_device(): factor = lax.all_gather(thc_factor, ROW_COL, axis=1, tiled=True)]
    pallas_call x0 -> x1, Pallas kernels: none -> 85.9 us  [per_device(): pl.pallas_call(kernel, out_shape=jax.ShapeDtypeStruct((256, 512), BF), in...]
    all_to_all x3 -> x0, starting transfers between devices: 34.8 us -> none  [the longest x1 14.5 us: sent_to_all(): lax.all_to_all(jnp.broadcast_to(shard[None], (count, *shard.shape)), axis...]
    all_to_all x3 -> x0, waiting for transfers between devices: 30.9 us -> none  [the longest x1 20.9 us: exchange_both(): lax.all_to_all(pieces, axis, split_axis=0, concat_axis=0, tiled=True)]
    all_to_all x1 -> x0, blocking collectives: 15.6 us -> none  [per_device(): lax.all_to_all(sectioned_back, ROW, split_axis=1, concat_axis=3, tiled=True)]
    all_gather x1 -> x0, blocking collectives: 10.7 us -> none  [gather_in_order(): pieces = lax.all_gather(pieces, axes[k], axis=0, tiled=True)]
    dot_general x4 -> x0, matrix products: 10.1 us -> none  [the longest x1 4.22 us: per_device(): jnp.dot(gathered_by_axis(hh_coupling, ROW, (0, 1), 0), amplitudes, prefer...]
  transfers between devices with their start and end apart: 5 -> 0, of which waited for: 3 -> 0; matrix products, arithmetic and copies ran while one was open for 3% -> 0% of each run, Pallas kernels for 0% -> 0%
where the time goes in v1:
time: 94.6 us; the launch traced here: 94.3 us
  Pallas kernels  85.9 us (91%)
  local copies, waits for them, and re-layouts  8.28 us (9%)
    pallas_call x1, Pallas kernels, per_device(): pl.pallas_call(kernel, out_shape=jax.ShapeDtypeStruct((256, 512), BF), in...  85.9 us
    unnamed x15, local copies, waits for them, and re-layouts  7.48 us

profile of v1, /device:TPU:1, one launch (start us, length us, event | category | flops | bytes accessed | tf_op | source)
XLA Modules:
  0.0 94.3 jit_solution(9772334499952574536)
XLA Ops:
  0.0 0.8 copy.9.owner
  0.8 0.0 copy-start
  0.8 2.2 %copy-done = bf16[4096,512]{1,0:T(8,128)(2,1)S(1)} copy-done((bf16[4096,512]{1,0:T(8,128)(2,1)S(1)}, bf16[4096,512]{1,0:T(8,128)(2,1)}, u32[]{:S(2)}) %copy-start) | copy-done | bytes 4194328
  3.0 0.0 copy-start.1
  3.0 0.9 %copy-done.1 = bf16[256,512]{1,0:T(8,128)(2,1)S(1)} copy-done((bf16[256,512]{1,0:T(8,128)(2,1)S(1)}, bf16[256,512]{1,0:T(8,128)(2,1)}, u32[]{:S(2)}) %copy-start.1) | copy-done | bytes 262168
  4.0 0.0 copy-start.2
  4.0 0.9 copy-done.2
  4.9 0.0 copy-start.3
  4.9 0.7 copy-done.3
  5.6 0.0 copy-start.4
  5.6 0.7 copy-done.4
  6.3 0.0 copy-start.5
  6.3 0.7 copy-done.5
  6.9 0.0 copy-start.6
  6.9 0.7 copy-done.6
  7.6 85.9 %shard_map.82 = bf16[256,512]{1,0:T(8,128)(2,1)S(1)} custom-call(bf16[4096,512]{1,0:T(8,128)(2,1)S(1)} %copy-done, bf16[256,512]{1,0:T(8,128)(2,1)S(1)} %copy-done.1, bf16[16,4096]{1,0:T(8,128)(2,1)S(1)} %copy-done.2, bf16[2,512]{1,0:T(2,128)(2,1)S(1)} %bitcast.4, f32[32,64]{1,0:T(8,128)S(1)} %copy-done.3, f32[1,64]{1,0:T(1,128)S(1)} %bitcast.6, ...), custom_call_target="tpu_custom_call" | custom-call | tf_op jit(solution)/shard_map/pallas_call | solution.py:497
  93.6 0.7 copy.11
Async XLA Ops:
  0.8 2.2 %copy-start = (bf16[4096,512]{1,0:T(8,128)(2,1)S(1)}, bf16[4096,512]{1,0:T(8,128)(2,1)}, u32[]{:S(2)}) copy-start(bf16[4096,512]{1,0:T(8,128)(2,1)} %amp_hbm.1) | copy-start | bytes 12582916
  3.0 0.9 %copy-start.1 = (bf16[256,512]{1,0:T(8,128)(2,1)S(1)}, bf16[256,512]{1,0:T(8,128)(2,1)}, u32[]{:S(2)}) copy-start(bf16[256,512]{1,0:T(8,128)(2,1)} %integrals.1) | copy-start | bytes 786436
  4.0 0.9 copy-start.2
  4.9 0.7 copy-start.3
  5.6 0.7 copy-start.4
  6.3 0.7 copy-start.5
  6.9 0.7 copy-start.6

commit v2 on v1

v2 whole, which is shorter than its diff:
```python
import jax
import jax.numpy as jnp
from jax import lax
from jax.experimental import pallas as pl
from jax.experimental.pallas import tpu as pltpu
from jax.sharding import Mesh
from jax.sharding import PartitionSpec as P

AXES = ("zl", "y", "x", "zh", "core")
ROW = ("zl", "y")
COL = ("x", "zh", "core")
BF = jnp.bfloat16
F32 = jnp.float32
N_MOVES = 51


def nt(a, b):
    return lax.dot_general(a, b, (((1,), (1,)), ((), ())), preferred_element_type=F32)


def nn(a, b):
    return jnp.dot(a, b, preferred_element_type=F32)


def iota(shape, dim):
    return lax.broadcasted_iota(jnp.int32, shape, dim)


def swap_matrix():
    i, j = iota((256, 256), 0), iota((256, 256), 1)
    return (j == (i % 16) * 16 + i // 16).astype(F32).astype(BF)


def order_matrix():
    p, c = iota((512, 512), 0), iota((512, 512), 1)
    return (c == (p % 16) * 32 + ((p // 16) % 16) * 2 + p // 256).astype(F32).astype(BF)


def remote(src, dst, sems, slot, where):
    return pltpu.make_async_remote_copy(
        src_ref=src,
        dst_ref=dst,
        send_sem=sems[0].at[slot],
        recv_sem=sems[1].at[slot],
        device_id=where,
        device_id_type=pl.DeviceIdType.MESH,
    )


class Exchange:
    def __init__(self, sems, slot, count, me, where, src, dst, rest):
        self.sems, self.slot, self.count, self.me = sems, slot, count, me
        self.where, self.src, self.dst, self.rest = where, src, dst, rest

    def start(self):
        def step(d, carry):
            to = lax.rem(self.me + d, self.count)
            remote(
                self.src(to), self.dst(self.me), self.sems, self.slot, self.where(to)
            ).start()
            return carry

        lax.fori_loop(1, self.count, step, 0)

    def everything(self):
        to = lax.rem(self.me + 1, self.count)
        return remote(self.rest, self.rest, self.sems, self.slot, self.where(to))

    def wait_recv(self):
        self.everything().wait_recv()

    def wait_send(self):
        self.everything().wait_send()


class RingOfFour:
    def __init__(self, sems, slot, me, block, half):
        self.sems, self.slot = sems, slot
        self.me, self.right, self.across, self.left = (lax.rem(me + d, 4) for d in range(4))
        self.block, self.half = block, half

    def copy(self, part, ref, to):
        return remote(ref, ref, self.sems, self.slot + part, {"x": to})

    def start(self):
        self.copy(0, self.block(self.me), self.right).start()
        self.copy(1, self.block(self.me), self.left).start()

    def forward(self):
        self.copy(0, self.block(self.left), self.right).wait_recv()
        self.copy(2, self.half(self.left, 0), self.right).start()
        self.copy(1, self.block(self.right), self.left).wait_recv()
        self.copy(3, self.half(self.right, 1), self.left).start()

    def wait_recv(self):
        self.copy(2, self.half(self.across, 0), self.right).wait_recv()
        self.copy(3, self.half(self.across, 1), self.left).wait_recv()

    def wait_send(self):
        self.copy(0, self.block(self.me), self.right).wait_send()
        self.copy(1, self.block(self.me), self.left).wait_send()
        self.copy(2, self.half(self.left, 0), self.right).wait_send()
        self.copy(3, self.half(self.right, 1), self.left).wait_send()


class Swap:
    def __init__(self, sems, slot, core, src, dst):
        self.sems, self.slot, self.core = sems, slot, core
        self.src, self.dst = src, dst

    def copy(self, place):
        return remote(
            self.src, self.dst(place), self.sems, self.slot, {"core": 1 - self.core}
        )

    def start(self):
        self.copy(self.core).start()

    def wait_recv(self):
        self.copy(1 - self.core).wait_recv()

    def wait_send(self):
        self.copy(self.core).wait_send()


def kernel(
    amp_hbm, integrals_hbm, hh_hbm, factor_hbm, core_hbm, occ_hbm, vir_hbm, owner_hbm, out_hbm,
    amp, integrals, hh, factor, core_in, occ, vir, owner_row, out,
    own, own0, own1, in0, in1, mid0, mid1, fin0, fin1, whole,
    chunk, pieces, points, core_parts, rows, half, order0, order1, middle, weighted,
    give, take, lad0, lad1, got0, got1, turn0, turn1, back0, back1,
    coupled, in_sems, out_sems, send_sems, recv_sems,
):
    zl, y, x, zh, core = (lax.axis_index(a) for a in AXES)
    r, xz = zl * 8 + y, x * 4 + zh
    other = 1 - core
    sems = (send_sems, recv_sems)
    MESH = pl.DeviceIdType.MESH

    def row_at(t):
        return {"zl": t // 8, "y": t % 8}

    def col_at(t):
        return {"x": t // 4, "zh": t % 4}

    fetches = [
        pltpu.make_async_copy(src, dst, in_sems.at[k])
        for k, (src, dst) in enumerate(
            (
                (factor_hbm, factor),
                (core_hbm, core_in),
                (hh_hbm, hh),
                (owner_hbm, owner_row),
                (amp_hbm, amp),
                (occ_hbm, occ),
                (vir_hbm, vir),
                (integrals_hbm, integrals),
            )
        )
    ]
    for fetch in fetches[:4]:
        fetch.start()

    barrier = pltpu.get_barrier_semaphore()

    def greet(d, carry):
        pl.semaphore_signal(
            barrier, inc=1, device_id=row_at(lax.rem(r + d, 16)), device_id_type=MESH
        )
        pl.semaphore_signal(
            barrier, inc=1, device_id=col_at(lax.rem(xz + d, 16)), device_id_type=MESH
        )
        return carry

    lax.fori_loop(1, 16, greet, 0)
    for d in range(4):
        pl.semaphore_signal(
            barrier,
            inc=1,
            device_id={"zh": lax.rem(zh + d, 4), "core": other},
            device_id_type=MESH,
        )
    for fetch in fetches[4:]:
        fetch.start()

    swap = swap_matrix()
    for fetch in fetches[:4]:
        fetch.wait()
    for k in range(2):
        chunk[k] = factor[:, k * 256 : k * 256 + 256].astype(F32)
    pieces[zh, core] = chunk[core]
    core_parts[x, zh, r] = jnp.concatenate(
        [core_in[0:16, :], core_in[16:32, :]], axis=1
    ).astype(BF)
    rows[core, x, r] = hh[:, pl.ds(pl.multiple_of((core * 4 + x) * 512, 512), 512)]
    owner = jnp.sum(
        jnp.where(iota((256, 256), 0) == iota((256, 256), 1), owner_row[...], 0),
        axis=1,
        keepdims=True,
    )

    fetches[4].wait()
    coupled[...] = jnp.zeros((256, 512), F32)

    def pick(k, carry):
        hit = owner == iota((256, 512), 1) + k * 512
        coupled[...] += nn(
            hit.astype(F32).astype(BF), amp[pl.ds(pl.multiple_of(k * 512, 512), 512), :]
        )
        return carry

    lax.fori_loop(0, 8, pick, 0)
    own[...] = coupled[...].astype(BF)
    own0[...] = own[:, :256].reshape(16, 16, 256)
    own1[...] = nn(swap, own[:, 256:]).astype(BF).reshape(16, 16, 256)
    in0[r] = own0[r]
    in1[xz] = own1[xz]

    first15 = pl.ds(0, 15)

    def row_exchange(slot, src, dst, rest):
        return Exchange(sems, slot, 16, r, row_at, src, dst, rest)

    def col_exchange(slot, src, dst, rest):
        return Exchange(sems, slot, 16, xz, col_at, src, dst, rest)

    def block_exchange(make, slot, src, dst):
        return make(slot, lambda t: src.at[t], lambda s: dst.at[s], dst.at[first15])

    amp0_row = block_exchange(row_exchange, 0, own0, in0)
    amp1_col = block_exchange(col_exchange, 1, own1, in1)
    amp0_col = block_exchange(col_exchange, 2, mid0, fin0)
    amp1_row = block_exchange(row_exchange, 3, mid1, fin1)
    lad0_col = block_exchange(col_exchange, 4, lad0, got0)
    lad1_row = block_exchange(row_exchange, 5, lad1, got1)
    lad0_row = block_exchange(row_exchange, 6, turn0, back0)
    lad1_col = block_exchange(col_exchange, 7, turn1, back1)
    core_row = row_exchange(
        8,
        lambda t: core_parts.at[x, zh, r],
        lambda s: core_parts.at[x, zh, s],
        core_parts.at[x, zh, first15],
    )
    fac_row = row_exchange(
        9,
        lambda t: points.at[core, r, x],
        lambda s: points.at[core, s, x],
        points.at[core, first15, x],
    )
    hh_row = row_exchange(
        10,
        lambda t: rows.at[core, x, r],
        lambda s: rows.at[core, x, s],
        rows.at[core, x, first15],
    )
    fac_swap = Swap(sems, 11, core, points.at[core], lambda s: points.at[s])
    hh_swap = Swap(sems, 12, core, rows.at[core], lambda s: rows.at[s])
    amp_swap = Swap(sems, 13, core, whole.at[core], lambda s: whole.at[s])
    lad_swap = Swap(sems, 14, core, give, lambda s: take)
    fac_x = RingOfFour(
        sems,
        15,
        x,
        lambda t: points.at[core, :, t],
        lambda t, h: points.at[core, pl.ds(h * 8, 8), t],
    )
    hh_x = RingOfFour(
        sems, 19, x, lambda t: rows.at[core, t], lambda t, h: rows.at[core, t, pl.ds(h * 8, 8)]
    )

    def core_ring(d):
        z = lax.rem(zh + 4 - d, 4)
        return RingOfFour(
            sems,
            23 + 4 * d,
            x,
            lambda t: core_parts.at[t, z],
            lambda t, h: core_parts.at[t, z, pl.ds(h * 8, 8)],
        )

    core_rings = [core_ring(d) for d in range(4)]

    def core_zh(d, place):
        part = core_parts.at[x, place]
        return remote(part, part, sems, 39 + d, {"zh": lax.rem(zh + d, 4)})

    def core_zh_in(d):
        return core_zh(d, lax.rem(zh + 4 - d, 4))

    def piece(d, c, to_zh, to_core, slot_zh, slot_core):
        return remote(
            chunk.at[to_core],
            pieces.at[slot_zh, slot_core],
            sems,
            43 + d * 2 + c,
            {"zh": to_zh, "core": to_core},
        )

    hops = [(d, c) for d in range(4) for c in range(2) if d or c]

    def piece_out(d, c):
        return piece(d, c, lax.rem(zh + d, 4), core if c == 0 else other, zh, core)

    def piece_in(d, c):
        from_zh, from_core = lax.rem(zh + 4 - d, 4), core if c == 0 else other
        return piece(d, c, from_zh, from_core, from_zh, from_core)

    pl.semaphore_wait(barrier, 34)
    for d, c in hops:
        piece_out(d, c).start()
    core_row.start()
    amp0_row.start()
    amp1_col.start()
    order = order_matrix()

    for d, c in hops:
        piece_in(d, c).wait_recv()
    point = iota((16, 256), 0)
    tile16 = jnp.zeros((16, 256), F32)
    for a in range(4):
        for b in range(2):
            for j in range(2):
                tile16 = jnp.where(
                    point == a * 4 + b * 2 + j, pieces[a, b, pl.ds(j, 1), :], tile16
                )
    points[core, r, x] = tile16.astype(BF)
    fac_row.start()

    core_row.wait_recv()
    for d in (1, 3, 2):
        core_zh(d, zh).start()
    core_rings[0].start()

    amp0_row.wait_recv()
    mid0[...] = nn(swap, in0[...].reshape(256, 256)).astype(BF).reshape(16, 16, 256)
    amp0_col.start()
    fin0[xz] = mid0[xz]
    amp1_col.wait_recv()
    mid1[...] = nn(swap, in1[...].reshape(256, 256)).astype(BF).reshape(16, 16, 256)
    amp1_row.start()
    fin1[r] = mid1[r]

    fac_row.wait_recv()
    fac_x.start()
    hh_row.start()
    core_zh_in(1).wait_recv()
    core_rings[1].start()
    core_zh_in(3).wait_recv()
    core_rings[3].start()
    fac_x.forward()
    core_zh_in(2).wait_recv()
    core_rings[2].start()

    amp0_col.wait_recv()
    whole[core, :, :256] = fin0[...].reshape(256, 256)
    amp1_row.wait_recv()
    whole[core, :, 256:] = nn(swap, fin1[...].reshape(256, 256)).astype(BF)
    amp_swap.start()

    core_rings[0].forward()
    core_rings[1].forward()
    fac_x.wait_recv()
    fac_swap.start()
    core_rings[3].forward()
    core_rings[2].forward()
    hh_row.wait_recv()
    hh_x.start()
    amp_swap.wait_recv()
    fac_swap.wait_recv()

    def my_points(h):
        return points[h, :, pl.ds(core * 2, 2)].reshape(512, 256)

    for h in range(4):
        at = pl.ds(h * 4, 4)
        got = nt(whole[...].reshape(512, 512)[:, :256], points[0, at].reshape(256, 256))
        got += nt(whole[...].reshape(512, 512)[:, 256:], points[1, at].reshape(256, 256))
        half[:, h * 256 : h * 256 + 256] = got.astype(BF)
    order0[...] = (nt(my_points(0), order[:, :256]) + nt(my_points(1), order[:, 256:])).astype(BF)
    order1[...] = (nt(order[:, :256], my_points(0)) + nt(order[:, 256:], my_points(1))).astype(BF)
    for t in range(4):
        cols = slice(t * 256, t * 256 + 256)
        middle[:, :, :, cols] = nn(order0[...], half[:, cols]).reshape(16, 2, 16, 256)

    low = iota((64, 128), 1) < 64

    def weigh(block):
        at = pl.ds(block * 4, 4)
        for t in range(8):
            cols = slice(t * 128, t * 128 + 128)
            even = core_parts[block, :, 2 * t].reshape(64, 128).astype(F32)
            odd = core_parts[block, :, 2 * t + 1].reshape(64, 128).astype(F32)
            top = jnp.where(low, even, pltpu.roll(odd, 64, 1)).reshape(4, 16, 128)
            bottom = jnp.where(low, pltpu.roll(even, 64, 1), odd).reshape(4, 16, 128)
            weighted[at, 0, :, cols] = (top * middle[at, 0, :, cols]).astype(BF)
            weighted[at, 1, :, cols] = (bottom * middle[at, 1, :, cols]).astype(BF)

    def weigh_near(i, carry):
        weigh(lax.rem(x + i + i // 2, 4))
        return carry

    lax.fori_loop(0, 3, weigh_near, 0)
    for ring in core_rings:
        ring.wait_recv()
    weigh(lax.rem(x + 2, 4))

    def contract(side):
        at = pl.ds(pl.multiple_of(side * 256, 256), 256)
        back = nn(order1[at, :], weighted[...].reshape(512, 1024)).astype(BF)
        return [nn(back, points[h].reshape(1024, 256)) for h in range(2)]

    give0, give1 = contract(other)
    give[:, :256] = give0.astype(BF)
    give[:, 256:] = give1.astype(BF)
    lad_swap.start()
    mine0, mine1 = contract(core)
    hh_x.forward()
    lad_swap.wait_recv()
    lad0[...] = (mine0 + take[:, :256].astype(F32)).astype(BF).reshape(16, 16, 256)
    lad0_col.start()
    mine1 = (mine1 + take[:, 256:].astype(F32)).astype(BF)
    lad1[...] = nn(swap, mine1).astype(BF).reshape(16, 16, 256)
    lad1_row.start()
    got0[xz] = lad0[xz]
    got1[r] = lad1[r]
    hh_x.wait_recv()
    hh_swap.start()

    lad0_col.wait_recv()
    turn0[...] = nn(swap, got0[...].reshape(256, 256)).astype(BF).reshape(16, 16, 256)
    lad0_row.start()
    back0[r] = turn0[r]
    lad1_row.wait_recv()
    turn1[...] = nn(swap, got1[...].reshape(256, 256)).astype(BF).reshape(16, 16, 256)
    lad1_col.start()
    back1[xz] = turn1[xz]

    hh_swap.wait_recv()
    coupled[...] = jnp.zeros((256, 512), F32)

    def couple(k, carry):
        coupled[...] += nn(
            rows[k // 4, k % 4].reshape(256, 512),
            amp[pl.ds(pl.multiple_of(k * 512, 512), 512), :],
        )
        return carry

    lax.fori_loop(0, 8, couple, 0)
    for fetch in fetches[5:]:
        fetch.wait()
    device = r * 32 + xz * 2 + core
    vir_mine = jnp.sum(
        jnp.where(iota((1, 512), 1) == device, vir[...], 0.0), axis=1, keepdims=True
    )
    orbital = iota((256, 64), 1)
    first_hit = (owner // 64) == orbital
    second_hit = (owner % 64) == orbital
    occ_first = jnp.sum(jnp.where(first_hit, occ[...], 0.0), axis=1, keepdims=True)
    occ_second = jnp.sum(jnp.where(second_hit, occ[...], 0.0), axis=1, keepdims=True)
    occ_pair = occ_first + occ_second
    coupled[...] += integrals[...].astype(F32)

    def finish(k, lad):
        cols = slice(k * 256, k * 256 + 256)
        denom = (vir_mine + vir[:, cols]) - occ_pair
        rest = coupled[:, cols] + lad.astype(F32)
        update = 0.4 * own[:, cols].astype(F32) + 0.6 * rest / denom
        out[:, cols] = update.astype(BF)
        done = pltpu.make_async_copy(out.at[:, cols], out_hbm.at[:, cols], out_sems.at[k])
        done.start()
        return done

    lad0_row.wait_recv()
    done0 = finish(0, back0[...].reshape(256, 256))
    lad1_col.wait_recv()
    done1 = finish(1, nn(swap, back1[...].reshape(256, 256)))

    for d, c in hops:
        piece_out(d, c).wait_send()
    for d in (1, 2, 3):
        core_zh(d, zh).wait_send()
    for move in (
        core_row, *core_rings, fac_row, fac_x, fac_swap, hh_row, hh_x, hh_swap,
        amp0_row, amp1_col, amp0_col, amp1_row, amp_swap, lad_swap,
        lad0_col, lad1_row, lad0_row, lad1_col,
    ):
        move.wait_send()
    done0.wait()
    done1.wait()


def per_device(
    amplitudes, integrals, hh_coupling, thc_factor, thc_core, occ_energy, vir_energy, pair_owner
):
    cube = pltpu.VMEM((16, 16, 256), BF)
    scratch = [
        pltpu.VMEM((4096, 512), BF),
        pltpu.VMEM((256, 512), BF),
        pltpu.VMEM((16, 4096), BF),
        pltpu.VMEM((2, 512), BF),
        pltpu.VMEM((32, 64), F32),
        pltpu.VMEM((1, 64), F32),
        pltpu.VMEM((1, 512), F32),
        pltpu.VMEM((1, 256), jnp.int32),
        pltpu.VMEM((256, 512), BF),
        pltpu.VMEM((256, 512), BF),
        *[cube] * 8,
        pltpu.VMEM((2, 256, 512), BF),
        pltpu.VMEM((2, 2, 256), F32),
        pltpu.VMEM((4, 2, 2, 256), F32),
        pltpu.VMEM((2, 16, 4, 16, 256), BF),
        pltpu.VMEM((4, 4, 16, 16, 128), BF),
        pltpu.VMEM((2, 4, 16, 16, 512), BF),
        pltpu.VMEM((512, 1024), BF),
        pltpu.VMEM((512, 512), BF),
        pltpu.VMEM((512, 512), BF),
        pltpu.VMEM((16, 2, 16, 1024), F32),
        pltpu.VMEM((16, 2, 16, 1024), BF),
        pltpu.VMEM((256, 512), BF),
        pltpu.VMEM((256, 512), BF),
        *[cube] * 8,
        pltpu.VMEM((256, 512), F32),
        pltpu.SemaphoreType.DMA((8,)),
        pltpu.SemaphoreType.DMA((2,)),
        pltpu.SemaphoreType.DMA((N_MOVES,)),
        pltpu.SemaphoreType.DMA((N_MOVES,)),
    ]
    return pl.pallas_call(
        kernel,
        out_shape=jax.ShapeDtypeStruct((256, 512), BF),
        in_specs=[pl.BlockSpec(memory_space=pltpu.HBM)] * 8,
        out_specs=pl.BlockSpec(memory_space=pltpu.HBM),
        scratch_shapes=scratch,
        compiler_params=pltpu.CompilerParams(
            collective_id=0, has_side_effects=True, vmem_limit_bytes=67043328
        ),
    )(
        amplitudes,
        integrals,
        hh_coupling,
        thc_factor.T,
        thc_core,
        occ_energy.reshape(1, -1),
        vir_energy.reshape(1, -1),
        pair_owner.reshape(1, -1),
    )


def solution(mesh):
    finer = Mesh(mesh.devices.reshape(2, 8, 4, 4, 2), AXES)
    wide = P(None, ROW + COL)
    in_specs = (wide, wide, P(ROW, None), wide, P(COL, ROW), P(), P(), P())
    return jax.shard_map(
        per_device, mesh=finer, in_specs=in_specs, out_specs=wide, check_vma=False
    )
```

time: 94.6 us -> 67.7 us (0.72)
  Pallas kernels: 85.9 us -> 65.9 us
  local copies, waits for them, and re-layouts: 8.28 us -> 1.67 us
    pallas_call x1, Pallas kernels: 85.9 us -> 65.9 us  [per_device(): pl.pallas_call(kernel, out_shape=jax.ShapeDtypeStruct((256, 512), BF), in...]
    unnamed x15 -> x1, local copies, waits for them, and re-layouts: 7.48 us -> 1.67 us
where the time goes in v2:
time: 67.7 us; the launch traced here: 67.5 us
  Pallas kernels  65.9 us (97%)
  local copies, waits for them, and re-layouts  1.67 us (2%)
    pallas_call x1, Pallas kernels, per_device(): pl.pallas_call(kernel, out_shape=jax.ShapeDtypeStruct((256, 512), BF), in...  65.9 us
    unnamed x1, local copies, waits for them, and re-layouts  1.67 us

profile of v2, /device:TPU:1, one launch (start us, length us, event | category | flops | bytes accessed | tf_op | source)
XLA Modules:
  0.0 67.5 jit_solution(5124404197763395171)
XLA Ops:
  0.0 65.9 %shard_map.82 = bf16[256,512]{1,0:T(8,128)(2,1)} custom-call(bf16[4096,512]{1,0:T(8,128)(2,1)} %amp_hbm.1, bf16[256,512]{1,0:T(8,128)(2,1)} %integrals_hbm.1, bf16[16,4096]{1,0:T(8,128)(2,1)} %hh_hbm.1, bf16[2,512]{1,0:T(2,128)(2,1)} %bitcast.4, f32[32,64]{1,0:T(8,128)} %core_hbm.1, f32[1,64]{1,0:T(1,128)} %bitcast.7, f32[1,512]{1,0:T(1,128)} %bitcast.5, ...), custom_call_target="tpu_custom_call" | custom-call | tf_op jit(solution)/shard_map/pallas_call | solution.py:528
  65.9 1.7 %copy.10 = bf16[256,512]{1,0:T(8,128)(2,1)} copy(bf16[256,512]{1,0:T(8,128)(2,1)} %shard_map.82) | data formatting | bytes 524288

commit v3 on v2

--- a/solution.py
+++ b/solution.py
@@ -11,7 +11,7 @@
 COL = ("x", "zh", "core")
 BF = jnp.bfloat16
 F32 = jnp.float32
-N_MOVES = 51
+N_MOVES = 58
 
 
 def nt(a, b):
@@ -47,6 +47,20 @@
     )
 
 
+class Single:
+    def __init__(self, outgoing, incoming):
+        self.outgoing, self.incoming = outgoing, incoming
+
+    def start(self):
+        self.outgoing().start()
+
+    def wait_recv(self):
+        self.incoming().wait_recv()
+
+    def wait_send(self):
+        self.outgoing().wait_send()
+
+
 class Exchange:
     def __init__(self, sems, slot, count, me, where, src, dst, rest):
         self.sems, self.slot, self.count, self.me = sems, slot, count, me
@@ -124,12 +138,12 @@
 
 
 def kernel(
-    amp_hbm, integrals_hbm, hh_hbm, factor_hbm, core_hbm, occ_hbm, vir_hbm, owner_hbm, out_hbm,
-    amp, integrals, hh, factor, core_in, occ, vir, owner_row, out,
+    amp_hbm, integrals_hbm, hh_hbm, factor_hbm, core_hbm, occ_hbm, vir_hbm, owner_hbm, out,
+    amp, integrals, hh, factor, core_in, occ, vir, owner_row,
     own, own0, own1, in0, in1, mid0, mid1, fin0, fin1, whole,
-    chunk, pieces, points, core_parts, rows, half, order0, order1, middle, weighted,
+    chunk, pieces, points, core_parts, rows, half, order, order0, order1, half_part, part0, part1, middle, weighted,
     give, take, lad0, lad1, got0, got1, turn0, turn1, back0, back1,
-    coupled, in_sems, out_sems, send_sems, recv_sems,
+    coupled, in_sems, send_sems, recv_sems,
 ):
     zl, y, x, zh, core = (lax.axis_index(a) for a in AXES)
     r, xz = zl * 8 + y, x * 4 + zh
@@ -149,17 +163,20 @@
             (
                 (factor_hbm, factor),
                 (core_hbm, core_in),
+                (owner_hbm, owner_row),
                 (hh_hbm, hh),
-                (owner_hbm, owner_row),
-                (amp_hbm, amp),
                 (occ_hbm, occ),
                 (vir_hbm, vir),
                 (integrals_hbm, integrals),
             )
         )
     ]
-    for fetch in fetches[:4]:
+    for fetch in fetches[:3]:
         fetch.start()
+
+    def eighth(k):
+        at = pl.ds(pl.multiple_of(k * 512, 512), 512)
+        return pltpu.make_async_copy(amp_hbm.at[at], amp.at[at], in_sems.at[7 + k])
 
     barrier = pltpu.get_barrier_semaphore()
 
@@ -180,11 +197,13 @@
             device_id={"zh": lax.rem(zh + d, 4), "core": other},
             device_id_type=MESH,
         )
-    for fetch in fetches[4:]:
+    for k in range(8):
+        eighth(k).start()
+    for fetch in fetches[3:]:
         fetch.start()
 
     swap = swap_matrix()
-    for fetch in fetches[:4]:
+    for fetch in fetches[:3]:
         fetch.wait()
     for k in range(2):
         chunk[k] = factor[:, k * 256 : k * 256 + 256].astype(F32)
@@ -192,29 +211,23 @@
     core_parts[x, zh, r] = jnp.concatenate(
         [core_in[0:16, :], core_in[16:32, :]], axis=1
     ).astype(BF)
-    rows[core, x, r] = hh[:, pl.ds(pl.multiple_of((core * 4 + x) * 512, 512), 512)]
     owner = jnp.sum(
         jnp.where(iota((256, 256), 0) == iota((256, 256), 1), owner_row[...], 0),
         axis=1,
         keepdims=True,
     )
 
-    fetches[4].wait()
     coupled[...] = jnp.zeros((256, 512), F32)
 
     def pick(k, carry):
+        eighth(k).wait()
         hit = owner == iota((256, 512), 1) + k * 512
         coupled[...] += nn(
             hit.astype(F32).astype(BF), amp[pl.ds(pl.multiple_of(k * 512, 512), 512), :]
         )
         return carry
 
-    lax.fori_loop(0, 8, pick, 0)
-    own[...] = coupled[...].astype(BF)
-    own0[...] = own[:, :256].reshape(16, 16, 256)
-    own1[...] = nn(swap, own[:, 256:]).astype(BF).reshape(16, 16, 256)
-    in0[r] = own0[r]
-    in1[xz] = own1[xz]
+    lax.fori_loop(0, 5, pick, 0)
 
     first15 = pl.ds(0, 15)
 
@@ -253,10 +266,22 @@
         lambda s: rows.at[core, x, s],
         rows.at[core, x, first15],
     )
-    fac_swap = Swap(sems, 11, core, points.at[core], lambda s: points.at[s])
-    hh_swap = Swap(sems, 12, core, rows.at[core], lambda s: rows.at[s])
+
+    def fac_part(slot, d):
+        t = lax.rem(x + d, 4)
+        return Swap(sems, slot, core, points.at[core, :, t], lambda s: points.at[s, :, t])
+
+    def hh_part(slot, d):
+        t = lax.rem(x + d, 4)
+        return Swap(sems, slot, core, rows.at[core, t], lambda s: rows.at[s, t])
+
+    fac_swaps = [fac_part(slot, d) for d, slot in enumerate((11, 51, 52, 53))]
+    hh_swaps = [hh_part(slot, d) for d, slot in enumerate((12, 55, 56, 57))]
     amp_swap = Swap(sems, 13, core, whole.at[core], lambda s: whole.at[s])
-    lad_swap = Swap(sems, 14, core, give, lambda s: take)
+    lad_swaps = [
+        Swap(sems, slot, core, give.at[h], lambda s, h=h: take.at[h])
+        for h, slot in enumerate((14, 54))
+    ]
     fac_x = RingOfFour(
         sems,
         15,
@@ -280,41 +305,52 @@
 
     core_rings = [core_ring(d) for d in range(4)]
 
-    def core_zh(d, place):
-        part = core_parts.at[x, place]
-        return remote(part, part, sems, 39 + d, {"zh": lax.rem(zh + d, 4)})
-
-    def core_zh_in(d):
-        return core_zh(d, lax.rem(zh + 4 - d, 4))
-
-    def piece(d, c, to_zh, to_core, slot_zh, slot_core):
-        return remote(
-            chunk.at[to_core],
-            pieces.at[slot_zh, slot_core],
-            sems,
-            43 + d * 2 + c,
-            {"zh": to_zh, "core": to_core},
-        )
-
-    hops = [(d, c) for d in range(4) for c in range(2) if d or c]
-
-    def piece_out(d, c):
-        return piece(d, c, lax.rem(zh + d, 4), core if c == 0 else other, zh, core)
-
-    def piece_in(d, c):
-        from_zh, from_core = lax.rem(zh + 4 - d, 4), core if c == 0 else other
-        return piece(d, c, from_zh, from_core, from_zh, from_core)
+    def core_step(d):
+        def copy(place):
+            part = core_parts.at[x, place]
+            return remote(part, part, sems, 39 + d, {"zh": lax.rem(zh + d, 4)})
+
+        return Single(lambda: copy(zh), lambda: copy(lax.rem(zh + 4 - d, 4)))
+
+    core_zh = {d: core_step(d) for d in (1, 3, 2)}
+
+    def piece_step(d, c):
+        def copy(to_zh, to_core, slot_zh, slot_core):
+            return remote(
+                chunk.at[to_core],
+                pieces.at[slot_zh, slot_core],
+                sems,
+                43 + d * 2 + c,
+                {"zh": to_zh, "core": to_core},
+            )
+
+        peer = core if c == 0 else other
+        source = lax.rem(zh + 4 - d, 4)
+        return Single(
+            lambda: copy(lax.rem(zh + d, 4), peer, zh, core),
+            lambda: copy(source, peer, source, peer),
+        )
+
+    hops = [piece_step(d, c) for d in range(4) for c in range(2) if d or c]
 
     pl.semaphore_wait(barrier, 34)
-    for d, c in hops:
-        piece_out(d, c).start()
+    for hop in hops:
+        hop.start()
     core_row.start()
+    lax.fori_loop(5, 8, pick, 0)
+    own[...] = coupled[...].astype(BF)
+    own0[...] = own[:, :256].reshape(16, 16, 256)
+    own1[...] = nn(swap, own[:, 256:]).astype(BF).reshape(16, 16, 256)
     amp0_row.start()
     amp1_col.start()
-    order = order_matrix()
-
-    for d, c in hops:
-        piece_in(d, c).wait_recv()
+    in0[r] = own0[r]
+    in1[xz] = own1[xz]
+    fetches[3].wait()
+    rows[core, x, r] = hh[:, pl.ds(pl.multiple_of((core * 4 + x) * 512, 512), 512)]
+    order[...] = order_matrix()
+
+    for hop in hops:
+        hop.wait_recv()
     point = iota((16, 256), 0)
     tile16 = jnp.zeros((16, 256), F32)
     for a in range(4):
@@ -327,8 +363,8 @@
     fac_row.start()
 
     core_row.wait_recv()
-    for d in (1, 3, 2):
-        core_zh(d, zh).start()
+    for step in core_zh.values():
+        step.start()
     core_rings[0].start()
 
     amp0_row.wait_recv()
@@ -342,13 +378,16 @@
 
     fac_row.wait_recv()
     fac_x.start()
+    fac_swaps[0].start()
     hh_row.start()
-    core_zh_in(1).wait_recv()
+    core_zh[1].wait_recv()
     core_rings[1].start()
-    core_zh_in(3).wait_recv()
+    core_zh[3].wait_recv()
     core_rings[3].start()
     fac_x.forward()
-    core_zh_in(2).wait_recv()
+    fac_swaps[1].start()
+    fac_swaps[3].start()
+    core_zh[2].wait_recv()
     core_rings[2].start()
 
     amp0_col.wait_recv()
@@ -357,27 +396,40 @@
     whole[core, :, 256:] = nn(swap, fin1[...].reshape(256, 256)).astype(BF)
     amp_swap.start()
 
+    def my_points(h):
+        return points[h, :, pl.ds(core * 2, 2)].reshape(512, 256)
+
+    def lanes_half(h):
+        return pl.ds(pl.multiple_of(h * 256, 256), 256)
+
+    def half_from(h, t):
+        left = whole[:, :, lanes_half(h)].reshape(512, 256)
+        return nt(left, points[h, pl.ds(t * 4, 4)].reshape(256, 256))
+
     core_rings[0].forward()
     core_rings[1].forward()
     fac_x.wait_recv()
-    fac_swap.start()
+    fac_swaps[2].start()
     core_rings[3].forward()
+    amp_swap.wait_recv()
+
+    for t in range(4):
+        half_part[:, t * 256 : t * 256 + 256] = half_from(core, t)
+    part0[...] = nt(my_points(core), order[:, lanes_half(core)])
+    part1[...] = nt(order[:, lanes_half(core)], my_points(core))
+
     core_rings[2].forward()
     hh_row.wait_recv()
     hh_x.start()
-    amp_swap.wait_recv()
-    fac_swap.wait_recv()
-
-    def my_points(h):
-        return points[h, :, pl.ds(core * 2, 2)].reshape(512, 256)
-
-    for h in range(4):
-        at = pl.ds(h * 4, 4)
-        got = nt(whole[...].reshape(512, 512)[:, :256], points[0, at].reshape(256, 256))
-        got += nt(whole[...].reshape(512, 512)[:, 256:], points[1, at].reshape(256, 256))
-        half[:, h * 256 : h * 256 + 256] = got.astype(BF)
-    order0[...] = (nt(my_points(0), order[:, :256]) + nt(my_points(1), order[:, 256:])).astype(BF)
-    order1[...] = (nt(order[:, :256], my_points(0)) + nt(order[:, 256:], my_points(1))).astype(BF)
+    hh_swaps[0].start()
+    for part in fac_swaps:
+        part.wait_recv()
+
+    for t in range(4):
+        cols = slice(t * 256, t * 256 + 256)
+        half[:, cols] = (half_part[:, cols] + half_from(other, t)).astype(BF)
+    order0[...] = (part0[...] + nt(my_points(other), order[:, lanes_half(other)])).astype(BF)
+    order1[...] = (part1[...] + nt(order[:, lanes_half(other)], my_points(other))).astype(BF)
     for t in range(4):
         cols = slice(t * 256, t * 256 + 256)
         middle[:, :, :, cols] = nn(order0[...], half[:, cols]).reshape(16, 2, 16, 256)
@@ -404,27 +456,32 @@
         ring.wait_recv()
     weigh(lax.rem(x + 2, 4))
 
-    def contract(side):
+    def back_of(side):
         at = pl.ds(pl.multiple_of(side * 256, 256), 256)
-        back = nn(order1[at, :], weighted[...].reshape(512, 1024)).astype(BF)
-        return [nn(back, points[h].reshape(1024, 256)) for h in range(2)]
-
-    give0, give1 = contract(other)
-    give[:, :256] = give0.astype(BF)
-    give[:, 256:] = give1.astype(BF)
-    lad_swap.start()
-    mine0, mine1 = contract(core)
+        return nn(order1[at, :], weighted[...].reshape(512, 1024)).astype(BF)
+
+    def ladder_of(back, h):
+        return nn(back, points[h].reshape(1024, 256))
+
+    back = back_of(other)
+    for h in range(2):
+        give[h] = ladder_of(back, h).astype(BF)
+        lad_swaps[h].start()
+    back = back_of(core)
+    mine = ladder_of(back, 0)
+    lad_swaps[0].wait_recv()
+    lad0[...] = (mine + take[0].astype(F32)).astype(BF).reshape(16, 16, 256)
+    lad0_col.start()
+    mine = ladder_of(back, 1)
+    lad_swaps[1].wait_recv()
+    mine = (mine + take[1].astype(F32)).astype(BF)
+    lad1[...] = nn(swap, mine).astype(BF).reshape(16, 16, 256)
+    lad1_row.start()
     hh_x.forward()
-    lad_swap.wait_recv()
-    lad0[...] = (mine0 + take[:, :256].astype(F32)).astype(BF).reshape(16, 16, 256)
-    lad0_col.start()
-    mine1 = (mine1 + take[:, 256:].astype(F32)).astype(BF)
-    lad1[...] = nn(swap, mine1).astype(BF).reshape(16, 16, 256)
-    lad1_row.start()
+    hh_swaps[1].start()
+    hh_swaps[3].start()
     got0[xz] = lad0[xz]
     got1[r] = lad1[r]
-    hh_x.wait_recv()
-    hh_swap.start()
 
     lad0_col.wait_recv()
     turn0[...] = nn(swap, got0[...].reshape(256, 256)).astype(BF).reshape(16, 16, 256)
@@ -435,7 +492,10 @@
     lad1_col.start()
     back1[xz] = turn1[xz]
 
-    hh_swap.wait_recv()
+    hh_x.wait_recv()
+    hh_swaps[2].start()
+    for part in hh_swaps:
+        part.wait_recv()
     coupled[...] = jnp.zeros((256, 512), F32)
 
     def couple(k, carry):
@@ -446,7 +506,7 @@
         return carry
 
     lax.fori_loop(0, 8, couple, 0)
-    for fetch in fetches[5:]:
+    for fetch in fetches[4:]:
         fetch.wait()
     device = r * 32 + xz * 2 + core
     vir_mine = jnp.sum(
@@ -466,27 +526,18 @@
         rest = coupled[:, cols] + lad.astype(F32)
         update = 0.4 * own[:, cols].astype(F32) + 0.6 * rest / denom
         out[:, cols] = update.astype(BF)
-        done = pltpu.make_async_copy(out.at[:, cols], out_hbm.at[:, cols], out_sems.at[k])
-        done.start()
-        return done
 
     lad0_row.wait_recv()
-    done0 = finish(0, back0[...].reshape(256, 256))
+    finish(0, back0[...].reshape(256, 256))
     lad1_col.wait_recv()
-    done1 = finish(1, nn(swap, back1[...].reshape(256, 256)))
-
-    for d, c in hops:
-        piece_out(d, c).wait_send()
-    for d in (1, 2, 3):
-        core_zh(d, zh).wait_send()
+    finish(1, nn(swap, back1[...].reshape(256, 256)))
+
     for move in (
-        core_row, *core_rings, fac_row, fac_x, fac_swap, hh_row, hh_x, hh_swap,
-        amp0_row, amp1_col, amp0_col, amp1_row, amp_swap, lad_swap,
+        *hops, *core_zh.values(), core_row, *core_rings, fac_row, fac_x, *fac_swaps, hh_row, hh_x, *hh_swaps,
+        amp0_row, amp1_col, amp0_col, amp1_row, amp_swap, *lad_swaps,
         lad0_col, lad1_row, lad0_row, lad1_col,
     ):
         move.wait_send()
-    done0.wait()
-    done1.wait()
 
 
 def per_device(
@@ -503,7 +554,6 @@
         pltpu.VMEM((1, 512), F32),
         pltpu.VMEM((1, 256), jnp.int32),
         pltpu.VMEM((256, 512), BF),
-        pltpu.VMEM((256, 512), BF),
         *[cube] * 8,
         pltpu.VMEM((2, 256, 512), BF),
         pltpu.VMEM((2, 2, 256), F32),
@@ -514,14 +564,17 @@
         pltpu.VMEM((512, 1024), BF),
         pltpu.VMEM((512, 512), BF),
         pltpu.VMEM((512, 512), BF),
+        pltpu.VMEM((512, 512), BF),
+        pltpu.VMEM((512, 1024), F32),
+        pltpu.VMEM((512, 512), F32),
+        pltpu.VMEM((512, 512), F32),
         pltpu.VMEM((16, 2, 16, 1024), F32),
         pltpu.VMEM((16, 2, 16, 1024), BF),
-        pltpu.VMEM((256, 512), BF),
-        pltpu.VMEM((256, 512), BF),
+        pltpu.VMEM((2, 256, 256), BF),
+        pltpu.VMEM((2, 256, 256), BF),
         *[cube] * 8,
         pltpu.VMEM((256, 512), F32),
-        pltpu.SemaphoreType.DMA((8,)),
-        pltpu.SemaphoreType.DMA((2,)),
+        pltpu.SemaphoreType.DMA((15,)),
         pltpu.SemaphoreType.DMA((N_MOVES,)),
         pltpu.SemaphoreType.DMA((N_MOVES,)),
     ]
@@ -529,20 +582,25 @@
         kernel,
         out_shape=jax.ShapeDtypeStruct((256, 512), BF),
         in_specs=[pl.BlockSpec(memory_space=pltpu.HBM)] * 8,
-        out_specs=pl.BlockSpec(memory_space=pltpu.HBM),
+        out_specs=pl.BlockSpec(memory_space=pltpu.VMEM),
         scratch_shapes=scratch,
         compiler_params=pltpu.CompilerParams(
-            collective_id=0, has_side_effects=True, vmem_limit_bytes=67043328
+            collective_id=0, has_side_effects=True, vmem_limit_bytes=50000000
         ),
     )(
-        amplitudes,
-        integrals,
-        hh_coupling,
-        thc_factor.T,
-        thc_core,
-        occ_energy.reshape(1, -1),
-        vir_energy.reshape(1, -1),
-        pair_owner.reshape(1, -1),
+        *(
+            pltpu.with_memory_space_constraint(operand, pltpu.HBM)
+            for operand in (
+                amplitudes,
+                integrals,
+                hh_coupling,
+                thc_factor.T,
+                thc_core,
+                occ_energy.reshape(1, -1),
+                vir_energy.reshape(1, -1),
+                pair_owner.reshape(1, -1),
+            )
+        )
     )
 
 

time: 67.7 us -> 65.2 us (0.963)
  Pallas kernels: 65.9 us -> 64.4 us
  local copies, waits for them, and re-layouts: 1.67 us -> 0.71 us
    pallas_call x1, Pallas kernels: 65.9 us -> 64.4 us  [per_device(): pl.pallas_call(kernel, out_shape=jax.ShapeDtypeStruct((256, 512), BF), in...]
    unnamed x1, local copies, waits for them, and re-layouts: 1.67 us -> 0.71 us
where the time goes in v3:
time: 65.2 us; the launch traced here: 65.1 us
  Pallas kernels  64.4 us (99%)
  local copies, waits for them, and re-layouts  0.71 us (1%)
    pallas_call x1, Pallas kernels, per_device(): pl.pallas_call(kernel, out_shape=jax.ShapeDtypeStruct((256, 512), BF), in...  64.4 us

profile of v3, /device:TPU:1, one launch (start us, length us, event | category | flops | bytes accessed | tf_op | source)
XLA Modules:
  0.0 65.1 jit_solution(11551642253923561959)
XLA Ops:
  0.0 64.4 %shard_map.82 = bf16[256,512]{1,0:T(8,128)(2,1)S(1)} custom-call(bf16[4096,512]{1,0:T(8,128)(2,1)} %amp_hbm.1, bf16[256,512]{1,0:T(8,128)(2,1)} %integrals_hbm.1, bf16[16,4096]{1,0:T(8,128)(2,1)} %hh_hbm.1, bf16[2,512]{1,0:T(2,128)(2,1)} %bitcast.4, f32[32,64]{1,0:T(8,128)} %core_hbm.1, f32[1,64]{1,0:T(1,128)} %bitcast.7, f32[1,512]{1,0:T(1,128)} %bitcast.5, ...), custom_call_target="tpu_custom_call" | custom-call | tf_op jit(solution)/shard_map/pallas_call | solution.py:581
  64.4 0.7 %copy.10 = bf16[256,512]{1,0:T(8,128)(2,1)} copy(bf16[256,512]{1,0:T(8,128)(2,1)S(1)} %shard_map.82) | data formatting | bytes 524288

commit v4 on v3

--- a/solution.py
+++ b/solution.py
@@ -379,14 +379,14 @@
     fac_row.wait_recv()
     fac_x.start()
     fac_swaps[0].start()
-    hh_row.start()
     core_zh[1].wait_recv()
     core_rings[1].start()
-    core_zh[3].wait_recv()
-    core_rings[3].start()
     fac_x.forward()
     fac_swaps[1].start()
     fac_swaps[3].start()
+    hh_row.start()
+    core_zh[3].wait_recv()
+    core_rings[3].start()
     core_zh[2].wait_recv()
     core_rings[2].start()
 

time: 65.2 us -> 66.1 us (1.014)
  Pallas kernels: 64.4 us -> 65.3 us
    pallas_call x1, Pallas kernels: 64.4 us -> 65.3 us  [per_device(): pl.pallas_call(kernel, out_shape=jax.ShapeDtypeStruct((256, 512), BF), in...]
where the time goes in v4:
time: 66.1 us; the launch traced here: 66 us
  Pallas kernels  65.3 us (99%)
  local copies, waits for them, and re-layouts  0.71 us (1%)
    pallas_call x1, Pallas kernels, per_device(): pl.pallas_call(kernel, out_shape=jax.ShapeDtypeStruct((256, 512), BF), in...  65.3 us

profile of v4, /device:TPU:1, one launch (start us, length us, event | category | flops | bytes accessed | tf_op | source)
XLA Modules:
  0.0 66.0 jit_solution(9673122979220002924)
XLA Ops:
  0.0 65.3 %shard_map.82 = bf16[256,512]{1,0:T(8,128)(2,1)S(1)} custom-call(bf16[4096,512]{1,0:T(8,128)(2,1)} %amp_hbm.1, bf16[256,512]{1,0:T(8,128)(2,1)} %integrals_hbm.1, bf16[16,4096]{1,0:T(8,128)(2,1)} %hh_hbm.1, bf16[2,512]{1,0:T(2,128)(2,1)} %bitcast.4, f32[32,64]{1,0:T(8,128)} %core_hbm.1, f32[1,64]{1,0:T(1,128)} %bitcast.7, f32[1,512]{1,0:T(1,128)} %bitcast.5, ...), custom_call_target="tpu_custom_call" | custom-call | tf_op jit(solution)/shard_map/pallas_call | solution.py:581
  65.3 0.7 %copy.10 = bf16[256,512]{1,0:T(8,128)(2,1)} copy(bf16[256,512]{1,0:T(8,128)(2,1)S(1)} %shard_map.82) | data formatting | bytes 524288
